TPU v7x, 32 devices: a whole 2x2x4 slice. The times are simulated.
32 devices in a mesh: lat: 4 (over z), lon: 8 (over y, x, core).
Axes of the slice: x: 2, y: 2, z: 4, core: 2. Of those that a mesh axis runs over, the one named last changes fastest.
Arguments:
- poleward_flow: float32 [10, 4, 256, 1024], P(None, None, 'lat', 'lon'), may hold values from -16 to 16
- potential_warmth: float32 [10, 4, 256, 1024], P(None, None, 'lat', 'lon'), may hold values from -16 to 16
- water_profile_flag: int32 [256, 1024], P('lat', 'lon'), may hold values from 0 to 1
- floor_count: int32 [256, 1024], P('lat', 'lon'), may hold values from 0 to 4, as said below
- catchment_label_for_site: int32 [256, 1024], P('lat', 'lon'), may hold values from 0 to 9
Outputs:
- eddy_temp: float32 [4, 256, 1024], P(None, 'lat', 'lon')
- transport: float32 [4, 10, 4, 256], P(None, None, None, ('lat', 'lon'))
Inputs may be any that keep to these rules, and one draw needn't show every extreme that they name: `floor_count`: land rows of zeros occur at some latitudes; elsewhere columns have 1 to 4 wet levels.
All inputs are finite; a program needn't handle non-finite values.
Results may differ from a plain program's by a relative error of at most 0.0003.
Values sent between devices are 32-bit elements; how exact they have to be, the bound alone decides.
A program may use at most 64 MiB of HBM per device.

v0:
```python
import math

import jax
import jax.numpy as jnp
from jax import lax
from jax.sharding import PartitionSpec as P

BASINS = 10


highest_accuracy = lax.Precision.HIGHEST


def shifted(block, axis, distance):
    devices = range(lax.axis_size(axis))
    route = [(i - distance, i) for i in devices if i - distance in devices]
    return lax.ppermute(block, axis, route)


def zonal_means(watered_total, along_latitude_totals):
    return along_latitude_totals / jnp.maximum(watered_total, 1.0)


def basin_cells(one_hot, per_basin):
    return jnp.einsum("bji,bkj->kji", one_hot, per_basin, precision=highest_accuracy)


def shards(
    poleward_flow, potential_warmth, water_profile_flag, floor_count, catchment_label_for_site
):
    snapshots, levels, lat_rows, lon_cols = poleward_flow.shape
    lon_devices = lax.axis_size("lon")
    share_rows = lat_rows // lon_devices
    row_start = lax.axis_index("lon") * share_rows
    scaling = 1.0 / math.sqrt(lon_cols * lon_devices)
    bottom_layer_limit = (water_profile_flag * floor_count).astype(jnp.float32)
    poleward_warmth, poleward_floor = shifted(
        (potential_warmth[:, :, 0, :], bottom_layer_limit[0]), "lat", -1
    )
    topmost_warmth = jnp.concatenate(
        [potential_warmth[:, :, 1:, :], poleward_warmth[:, :, None, :]], axis=2
    )
    warmth_entry = 0.5 * (potential_warmth + topmost_warmth)
    upper_depth = jnp.concatenate([bottom_layer_limit[1:], poleward_floor[None]], axis=0)
    level_values = jnp.arange(levels, dtype=jnp.float32)[:, None, None]
    wet_cells = (
        (level_values < bottom_layer_limit[None]) & (level_values < upper_depth[None])
    ).astype(jnp.float32)
    basin_ids = jnp.arange(BASINS, dtype=jnp.int32)
    one_hot = (catchment_label_for_site[None] == basin_ids[:, None, None]).astype(jnp.float32)
    scaling_factors = one_hot[:, None] * wet_cells[None]
    watered_total = jnp.sum(scaling_factors, axis=3)[None]
    along_latitude_flow = jnp.einsum(
        "yalq,falq->fyal", scaling_factors, poleward_flow, precision=highest_accuracy
    )
    along_latitude_warmth = jnp.einsum(
        "yalq,falq->fyal", scaling_factors, warmth_entry, precision=highest_accuracy
    )
    along_latitude_totals = jnp.concatenate([along_latitude_flow, along_latitude_warmth], axis=0)
    mean_velocity = jnp.mean(poleward_flow, axis=0)
    average_warmth = jnp.mean(warmth_entry, axis=0)
    cross_time = jnp.mean((poleward_flow - mean_velocity) * (warmth_entry - average_warmth), axis=0)
    product_sum = jnp.einsum(
        "bkji,kji->bkj", scaling_factors, mean_velocity * average_warmth, precision=highest_accuracy
    )
    cross_sum = jnp.einsum("bkji,kji->bkj", scaling_factors, cross_time, precision=highest_accuracy)
    stats = (watered_total, along_latitude_totals, jnp.stack([product_sum, cross_sum]))
    totals = lax.psum((stats[0], stats[1], stats[2]), "lon")
    own_stats = tuple(
        (lax.dynamic_slice_in_dim(member, row_start, share_rows, 3) for member in totals)
    )
    own_means = zonal_means(own_stats[0], own_stats[1])
    every_means = zonal_means(totals[0], totals[1])
    every_bar_temp = jnp.mean(every_means[snapshots:], axis=0)
    own_count = own_stats[0][0]
    own_bar_v = jnp.mean(own_means[:snapshots], axis=0)
    own_bar_t = jnp.mean(own_means[snapshots:], axis=0)
    mean_flow = scaling * own_count * own_bar_v * own_bar_t
    swing_product = jnp.mean(
        (own_means[:snapshots] - own_bar_v) * (own_means[snapshots:] - own_bar_t), axis=0
    )
    zonal_swing = scaling * own_count * swing_product
    averaged_warmth_grid = basin_cells(one_hot, every_bar_temp)
    temp_star = average_warmth - averaged_warmth_grid
    eddy_temp = wet_cells * temp_star
    steady_share = scaling * (own_stats[2][0] - own_count * own_bar_v * own_bar_t)
    transient = scaling * own_stats[2][1] - zonal_swing
    transport = jnp.stack([mean_flow, steady_share, zonal_swing, transient])
    return (eddy_temp, transport)


def solution(mesh):
    return jax.shard_map(
        shards,
        mesh=mesh,
        in_specs=(
            P(None, None, "lat", "lon"),
            P(None, None, "lat", "lon"),
            P("lat", "lon"),
            P("lat", "lon"),
            P("lat", "lon"),
        ),
        out_specs=(P(None, "lat", "lon"), P(None, None, None, ("lat", "lon"))),
        check_vma=False,
    )
```

profile of v0, /device:TPU:0, one launch (start us, length us, event | category | flops | bytes accessed | tf_op | source)
XLA Modules:
  0.0 108.0 jit_solution(1735994457637224425)
XLA Ops:
  7.2 1.0 slice.32
  8.3 1.3 %collective-permute-start.1 = (f32[10,4,128]{2,1,0:T(4,128)S(1)}, f32[10,4,128]{2,1,0:T(4,128)S(1)}, u32[]{:S(2)}, u32[]{:S(2)}) collective-permute-start(f32[10,4,128]{2,1,0:T(4,128)S(1)} %bitcast.58), channel_id=1, source_target_pairs={{8,0},{16,8},{24,16},{9,1},{17,9},{25,17},{10,2},{18,10},{26,18},{... | collective-permute-start | bytes 61448 | tf_op jit(solution)/shard_map/ppermute | solution.py:17
  9.6 0.8 multiply_convert_fusion
  10.3 1.3 %collective-permute-start = (f32[128]{0:T(128)S(1)}, f32[128]{0:T(128)S(1)}, u32[]{:S(2)}, u32[]{:S(2)}) collective-permute-start(f32[128]{0:T(128)S(1)} %slice_bitcast_fusion), channel_id=1, source_target_pairs={{8,0},{16,8},{24,16},{9,1},{17,9},{25,17},{10,2},{18,10},{26,18},{... | collective-permute-start | bytes 1544 | tf_op jit(solution)/shard_map/ppermute | solution.py:17
  11.6 2.5 %slice.31 = f32[10,4,63,128]{3,2,1,0:T(8,128)} slice(f32[10,4,64,128]{3,2,1,0:T(8,128)} %param.6), slice={[0:10], [0:4], [1:64], [0:128]} | slice | bytes 2580480 | tf_op jit(solution)/shard_map/slice | solution.py:41
  14.2 0.7 reduce_sum.77
  15.0 2.5 %collective-permute-done = f32[128]{0:T(128)S(1)} collective-permute-done((f32[128]{0:T(128)S(1)}, f32[128]{0:T(128)S(1)}, u32[]{:S(2)}, u32[]{:S(2)}) %collective-permute-start) | collective-permute-done | bytes 544 | tf_op jit(solution)/shard_map/ppermute | solution.py:17
  17.5 5.4 %fusion.10 = f32[10,10,4,64]{0,1,3,2:T(8,128)} fusion(f32[10,4,64,128]{3,2,1,0:T(8,128)S(1)} %copy-done, f32[4,64,128]{2,1,0:T(8,128)S(1)} %copy.72, f32[10,64,128]{2,0,1:T(8,128)S(1)} %fusion.31), kind=kOutput, calls=%fused_computation.11 | convolution fusion | flops 39649280 | bytes 1871872 | tf_op jit(solution)/shard_map/yalq,falq->fyal/dot_general | solution.py:53
  22.9 1.3 %multiply_reduce_fusion = f32[10,4,64]{0,2,1:T(8,128)} fusion(f32[4,64,128]{2,1,0:T(8,128)S(1)} %copy.72, f32[10,64,128]{2,0,1:T(8,128)S(1)} %fusion.31), kind=kLoop, calls=%fused_computation.4 | loop fusion | flops 652800 | bytes 468992 | tf_op jit(solution)/shard_map/reduce_sum | solution.py:52
  24.2 2.2 %copy.75 = f32[10,10,4,64]{3,2,1,0:T(4,128)S(1)} copy(f32[10,10,4,64]{0,1,3,2:T(8,128)} %fusion.10) | data formatting | bytes 204800 | tf_op jit(solution)/shard_map/yalq,falq->fyal/transpose | solution.py:53
  26.4 0.6 copy-done.5
  27.0 2.6 %fusion.40 = (f32[4,64,128]{2,1,0:T(8,128)}, f32[10,4,64,128]{3,2,1,0:T(8,128)S(1)}) fusion(f32[10,4,64,128]{3,2,1,0:T(8,128)} %param.6, f32[10,4,1,128]{3,2,1,0:T(1,128)} %bitcast.57, f32[10,4,63,128]{3,2,1,0:T(8,128)} %slice.31), kind=kLoop, calls=%fused_computation.67 | loop fusion | flops 1277952 | bytes 4063232 | tf_op jit(solution)/shard_map/reduce_sum | solution.py:61
  29.6 5.4 %fusion.15 = f32[10,10,4,64]{0,1,3,2:T(8,128)} fusion(f32[10,4,64,128]{3,2,1,0:T(8,128)S(1)} %get-tuple-element.19, f32[4,64,128]{2,1,0:T(8,128)S(1)} %copy.72, f32[10,64,128]{2,0,1:T(8,128)S(1)} %fusion.31), kind=kOutput, calls=%fused_computation.12 | convolution fusion | flops 39649280 | bytes 1871872 | tf_op jit(solution)/shard_map/yalq,falq->fyal/dot_general | solution.py:56
  35.0 2.9 %copy.76 = f32[10,10,4,64]{3,2,1,0:T(4,128)} copy(f32[10,10,4,64]{0,1,3,2:T(8,128)} %fusion.15) | data formatting | bytes 204800 | tf_op jit(solution)/shard_map/yalq,falq->fyal/transpose | solution.py:56
  37.9 1.8 %pad_maximum_fusion = f32[20,10,4,64]{3,2,1,0:T(4,128)} fusion(f32[10,10,4,64]{3,2,1,0:T(4,128)} %copy.76, f32[10,10,4,64]{3,2,1,0:T(4,128)S(1)} %copy.75), kind=kLoop, calls=%fused_computation.29 | loop fusion | flops 51200 | bytes 409600 | tf_op jit(solution)/shard_map/concatenate | solution.py:59
  39.7 1.2 %multiply_bitcast_fusion = (f32[4,64,128,1]{2,0,1,3:T(4,128)S(1)}, f32[4,64,128]{2,0,1:T(4,128)S(1)}, f32[4,64,128]{2,0,1:T(4,128)S(1)}) fusion(f32[4,64,128]{2,1,0:T(8,128)} %reduce_sum.77, f32[4,64,128]{2,1,0:T(8,128)} %get-tuple-element.18), kind=kLoop, calls=%fused_computation.42 | loop fusion | flops 98304 | bytes 655360 | tf_op jit(solution)/shard_map/mul | solution.py:64
  40.9 0.3 multiply_reduce_fusion.1
  41.4 3.6 %fusion = f32[4,64,1,10]{3,2,1,0:T(1,128)S(1)} fusion(f32[4,64,128]{2,1,0:T(8,128)S(1)} %copy.72, f32[10,64,128]{2,0,1:T(8,128)S(1)} %fusion.31, f32[4,64,128,1]{2,0,1,3:T(4,128)S(1)} %bitcast.54), kind=kOutput, calls=%fused_computation | convolution fusion | flops 4259840 | bytes 600064 | tf_op jit(solution)/shard_map/bkji,kji->bkj/dot_general | solution.py:66
  45.1 3.4 %fusion.2 = f32[4,64,1,10]{3,2,1,0:T(1,128)S(1)} fusion(f32[4,64,128]{2,1,0:T(8,128)S(1)} %copy.72, f32[10,64,128]{2,0,1:T(8,128)S(1)} %fusion.31, f32[4,64,128,1]{2,0,1,3:T(4,128)S(1)} %get-tuple-element.22), kind=kOutput, calls=%fused_computation.2 | convolution fusion | flops 4259840 | bytes 600064 | tf_op jit(solution)/shard_map/bkji,kji->bkj/dot_general | solution.py:63
  48.6 0.1 copy.88
  48.7 28.2 %all-reduce = (f32[1,10,4,64]{1,3,2,0:T(8,128)S(1)}, f32[2,10,4,64]{1,3,2,0:T(8,128)S(1)}) all-reduce(f32[1,10,4,64]{1,3,2,0:T(8,128)S(1)} %bitcast.53, f32[2,10,4,64]{1,3,2,0:T(8,128)S(1)} %copy.88), channel_id=1, replica_groups=mesh['lat'=4,'lon'=8] {'lon'}, use_global_device_ids=true, to_apply=%region_3.0 | all-reduce | flops 7680 | bytes 61440 | tf_op jit(solution)/shard_map/psum | solution.py:68
  76.9 0.1 copy.77
  77.0 0.1 copy.81
  77.1 19.0 %all-reduce.3.cloned.1.call-done = f32[20,10,4,64]{3,2,1,0:T(4,128)} async-done(((f32[20,10,4,64]{3,2,1,0:T(4,128)}), f32[20,10,4,64]{3,2,1,0:T(4,128)}) %all-reduce.3.cloned.1.call-update) | async-done | bytes 204816 | tf_op jit(solution)/shard_map/psum | solution.py:68
  96.2 1.0 fusion.33
  97.2 0.1 copy.80
  97.3 0.5 fusion.22
  97.8 0.7 copy.92
  98.5 1.3 %dynamic-slice_divide_fusion = f32[20,10,4,8]{3,2,1,0:T(4,128)S(1)} fusion(f32[20,10,4,64]{3,2,1,0:T(4,128)} %all-reduce.3.cloned.1.call-done, s32[]{:T(128)S(6)} %select_n.2, f32[10,4,8]{2,1,0:T(4,128)S(1)} %copy.81), kind=kLoop, calls=%fused_computation.30 | loop fusion | flops 6400 | bytes 52484 | tf_op jit(solution)/shard_map/div | solution.py:21
  99.9 0.1 copy.90
  100.4 0.1 copy.91
  100.5 0.6 pad_maximum_fusion.1
  (38 shorter events, 1.1 us)
Async XLA Ops:
  7.2 7.0 %copy-start.3 = (s32[64,128]{1,0:T(8,128)S(1)}, s32[64,128]{1,0:T(8,128)}, u32[]{:S(2)}) copy-start(s32[64,128]{1,0:T(8,128)} %param.9) | copy-start | bytes 98308
  7.2 7.1 %copy-start = (f32[10,4,64,128]{3,2,1,0:T(8,128)S(1)}, f32[10,4,64,128]{3,2,1,0:T(8,128)}, u32[]{:S(2)}) copy-start(f32[10,4,64,128]{3,2,1,0:T(8,128)} %param.5) | copy-start | bytes 3932164
  7.2 89.0 %all-reduce.3.cloned.1.call-start = ((), (), s32[]{:S(2)}) async-start(), calls=%async_computation | async-start | bytes 819200 | tf_op jit(solution)/shard_map/psum | solution.py:68
  8.3 18.2 %collective-permute-start.1 = (f32[10,4,128]{2,1,0:T(4,128)S(1)}, f32[10,4,128]{2,1,0:T(4,128)S(1)}, u32[]{:S(2)}, u32[]{:S(2)}) collective-permute-start(f32[10,4,128]{2,1,0:T(4,128)S(1)} %bitcast.58), channel_id=1, source_target_pairs={{8,0},{16,8},{24,16},{9,1},{17,9},{25,17},{10,2},{18,10},{26,18},{... | collective-permute-start | bytes 61448 | tf_op jit(solution)/shard_map/ppermute | solution.py:17
  10.3 7.1 %collective-permute-start = (f32[128]{0:T(128)S(1)}, f32[128]{0:T(128)S(1)}, u32[]{:S(2)}, u32[]{:S(2)}) collective-permute-start(f32[128]{0:T(128)S(1)} %slice_bitcast_fusion), channel_id=1, source_target_pairs={{8,0},{16,8},{24,16},{9,1},{17,9},{25,17},{10,2},{18,10},{26,18},{... | collective-permute-start | bytes 1544 | tf_op jit(solution)/shard_map/ppermute | solution.py:17
  26.4 0.6 copy-start.5
  41.2 7.5 %copy-start.2 = (f32[10,4,64]{0,2,1:T(8,128)S(1)}, f32[10,4,64]{0,2,1:T(8,128)}, u32[]{:S(2)}) copy-start(f32[10,4,64]{0,2,1:T(8,128)} %multiply_reduce_fusion) | copy-start | bytes 30724
  41.3 56.1 %copy-start.1 = (f32[4,64,128]{2,1,0:T(8,128)S(1)}, f32[4,64,128]{2,1,0:T(8,128)}, u32[]{:S(2)}) copy-start(f32[4,64,128]{2,1,0:T(8,128)} %get-tuple-element.18) | copy-start | bytes 393220
  41.3 56.1 %copy-start.4 = (s32[64,128]{1,0:T(8,128)S(1)}, s32[64,128]{1,0:T(8,128)}, u32[]{:S(2)}) copy-start(s32[64,128]{1,0:T(8,128)} %param.9) | copy-start | bytes 98308
Sparse Core Ops, SparseCore 0:
  39.8 56.3 all-reduce.2
where the time goes:
time: 108 us
  blocking collectives  28.2 us (26%)
  waiting for transfers between devices  21.5 us (20%)
  matrix products  18.2 us (17%)
  between operations  14.3 us (13%)
  other arithmetic  11.9 us (11%)
  local copies, waits for them, and re-layouts  11.3 us (10%)
  starting transfers between devices  2.62 us (2%)
    psum x1, blocking collectives, shards(): totals = lax.psum((stats[0], stats[1], stats[2]), 'lon')  28.2 us
    psum x1, waiting for transfers between devices, shards(): totals = lax.psum((stats[0], stats[1], stats[2]), 'lon')  19 us
    dot_general x1, matrix products, shards(): jnp.einsum('yalq,falq->fyal', scaling_factors, poleward_flow, precision=h...  5.38 us
    dot_general x1, matrix products, shards(): jnp.einsum('yalq,falq->fyal', scaling_factors, warmth_entry, precision=hi...  5.37 us
    dot_general x1, matrix products, shards(): jnp.einsum('bkji,kji->bkj', scaling_factors, cross_time, precision=highes...  3.56 us
    dot_general x1, matrix products, shards(): jnp.einsum('bkji,kji->bkj', scaling_factors, mean_velocity * average_warm...  3.4 us
    transpose x1, local copies, waits for them, and re-layouts, shards(): jnp.einsum('yalq,falq->fyal', scaling_factors, warmth_entry, precision=hi...  2.91 us
    reduce_sum x1, other arithmetic, shards(): average_warmth = jnp.mean(warmth_entry, axis=0)  2.58 us
  transfers between devices with their start and end apart: 3, of which 2 were waited for; matrix products, arithmetic and copies ran while one was open for 21% of the time, Pallas kernels for 0%

commit v1 on v0

v1 whole, which is shorter than its diff:
```python
import functools
import math

import jax
import jax.numpy as jnp
from jax import lax
from jax.experimental import pallas as pl
from jax.experimental.pallas import tpu as pltpu
from jax.sharding import PartitionSpec as P

BASINS = 10
MESH = pl.DeviceIdType.MESH
SUB = 8
LANES = 128


def kernel(
    lat_devices, lon_devices, snapshots, levels, share_rows,
    flow_hbm, warmth_hbm, flag_ref, floor_ref, label_ref,
    eddy_ref, transport_ref,
    flow, warmth, halo_flag, halo_floor, average, dots, stats, received, bars,
    load_flow, load_warmth, halo_send, halo_recv, stat_send, stat_recv, bar_send, bar_recv,
):
    rows = flow.shape[1]
    blocks = rows // SUB
    owners = SUB // share_rows
    planes = snapshots * levels
    lat = lax.axis_index("lat")
    me = lax.axis_index("lon")
    own_block = me // owners
    scaling = 1.0 / math.sqrt(LANES * lon_devices)

    def flow_copy(b):
        at = pl.ds(b * SUB, SUB)
        return pltpu.make_async_copy(flow_hbm.at[:, at, :], flow.at[:, at, :], load_flow.at[b])

    def warmth_copy(b):
        at = pl.ds(b * SUB, SUB)
        return pltpu.make_async_copy(warmth_hbm.at[:, at, :], warmth.at[:, at, :], load_warmth.at[b])

    for b in range(blocks):
        warmth_copy(b).start()
        flow_copy(b).start()

    barrier = pltpu.get_barrier_semaphore()
    for d in range(1, lon_devices):
        pl.semaphore_signal(
            barrier, inc=1, device_id=(lat, lax.rem(me + d, lon_devices)), device_id_type=MESH
        )

    @pl.when(lat > 0)
    def _():
        pl.semaphore_signal(barrier, inc=1, device_id=(lat - 1, me), device_id_type=MESH)

    @pl.when(lat < lat_devices - 1)
    def _():
        pl.semaphore_signal(barrier, inc=1, device_id=(lat + 1, me), device_id_type=MESH)

    greeted = lon_devices - 1 + (lat > 0).astype(jnp.int32) + (lat < lat_devices - 1).astype(jnp.int32)
    pl.semaphore_wait(barrier, greeted)

    halo_to = (jnp.maximum(lat - 1, 0), me)

    def halo_copies():
        pairs = (
            (warmth.at[:, pl.ds(0, 1), :], warmth.at[:, pl.ds(rows, 1), :]),
            (flag_ref.at[pl.ds(0, SUB), :], halo_flag),
            (floor_ref.at[pl.ds(0, SUB), :], halo_floor),
        )
        return [
            pltpu.make_async_remote_copy(
                src_ref=src, dst_ref=dst, send_sem=halo_send.at[n], recv_sem=halo_recv.at[n],
                device_id=halo_to, device_id_type=MESH,
            )
            for n, (src, dst) in enumerate(pairs)
        ]

    for b in range(blocks):
        warmth_copy(b).wait()
        if b == 0:
            @pl.when(lat > 0)
            def _():
                for copy in halo_copies():
                    copy.start()
        flow_copy(b).wait()

    @pl.when(lat < lat_devices - 1)
    def _():
        for copy in halo_copies():
            copy.wait_recv()

    @pl.when(lat == lat_devices - 1)
    def _():
        warmth[:, pl.ds(rows, 1), :] = jnp.zeros((planes, 1, LANES), jnp.float32)
        halo_flag[...] = jnp.zeros_like(halo_flag)
        halo_floor[...] = jnp.zeros_like(halo_floor)

    sub = lax.broadcasted_iota(jnp.int32, (SUB, LANES), 0)
    level = lax.broadcasted_iota(jnp.int32, (levels, SUB, LANES), 0)
    lane_row = lax.rem(lax.broadcasted_iota(jnp.int32, (SUB, LANES), 1), SUB)

    def next_row(here, after):
        first = lax.broadcasted_iota(jnp.int32, here.shape, here.ndim - 2) == 0
        return pltpu.roll(jnp.where(first, after, here), SUB - 1, here.ndim - 2)

    def wet_cells(b):
        at = pl.ds(pl.multiple_of(b * SUB, SUB), SUB)
        after = pl.ds(pl.multiple_of(lax.min(b + 1, blocks - 1) * SUB, SUB), SUB)
        depth = flag_ref[at, :] * floor_ref[at, :]
        inner = flag_ref[after, :] * floor_ref[after, :]
        outer = halo_flag[...] * halo_floor[...]
        limit = jnp.minimum(depth, next_row(depth, jnp.where(b == blocks - 1, outer, inner)))
        return (level < limit[None]).astype(jnp.float32)

    def stat_copy(b, g):
        return pltpu.make_async_remote_copy(
            src_ref=stats.at[b], dst_ref=received.at[me],
            send_sem=stat_send.at[b, g], recv_sem=stat_recv.at[me],
            device_id=(lat, b * owners + g), device_id_type=MESH,
        )

    def block_stats(s, carry):
        b = lax.rem(own_block + 1 + s, blocks)
        at = pl.ds(pl.multiple_of(b * SUB, SUB), SUB)
        after = pl.ds(pl.multiple_of(b * SUB + SUB, SUB), SUB)
        wet = wet_cells(b)
        velocity = flow[:, at, :].reshape(snapshots, levels, SUB, LANES)
        here = warmth[:, at, :]
        point = (0.5 * (here + next_row(here, warmth[:, after, :]))).reshape(
            snapshots, levels, SUB, LANES
        )
        mean_velocity = jnp.sum(velocity, axis=0) * (1.0 / snapshots)
        mean_warmth = jnp.sum(point, axis=0) * (1.0 / snapshots)
        cross = jnp.sum((velocity - mean_velocity) * (point - mean_warmth), axis=0) * (1.0 / snapshots)
        average[:, at, :] = mean_warmth
        fields = jnp.concatenate(
            [
                (velocity * wet[None]).reshape(planes, SUB, LANES),
                (point * wet[None]).reshape(planes, SUB, LANES),
                wet,
                wet,
                mean_velocity * mean_warmth * wet,
                cross * wet,
            ],
            axis=0,
        ).reshape(-1, LANES)
        high = fields.astype(jnp.bfloat16)
        low = (fields - high.astype(jnp.float32)).astype(jnp.bfloat16)
        labels = label_ref[at, :]
        member = jnp.concatenate(
            [(labels == n).astype(jnp.float32) for n in range(LANES // SUB)], axis=0
        ).astype(jnp.bfloat16)
        dots[...] = lax.dot_general(
            jnp.concatenate([high, low], axis=1), jnp.concatenate([member, member], axis=1),
            (((1,), (1,)), ((), ())), preferred_element_type=jnp.float32,
        )
        count = stats.shape[1]
        lanes = lax.rem(lax.broadcasted_iota(jnp.int32, (count, LANES), 1), SUB)
        gathered = dots[pl.ds(0, count, stride=SUB), :]
        for j in range(1, SUB):
            gathered = jnp.where(lanes == j, dots[pl.ds(j, count, stride=SUB), :], gathered)
        stats[pl.ds(b, 1)] = gathered[None]
        for g in range(owners):
            @pl.when(b * owners + g != me)
            def _():
                stat_copy(b, g).start()
        return carry

    lax.fori_loop(0, blocks, block_stats, 0)

    def add_received(d, total):
        src = lax.rem(me + lon_devices - d, lon_devices)
        pltpu.make_async_remote_copy(
            src_ref=stats.at[0], dst_ref=received.at[src],
            send_sem=stat_send.at[0, 0], recv_sem=stat_recv.at[src],
            device_id=(lat, src), device_id_type=MESH,
        ).wait_recv()
        return total + received[pl.ds(src, 1)][0]

    total = lax.fori_loop(1, lon_devices, add_received, stats[pl.ds(own_block, 1)][0])

    def both_halves(x):
        return x + pltpu.roll(x, levels, 0)

    count = total[2 * planes : 2 * planes + SUB]
    divisor = jnp.maximum(count, 1.0)
    means_v = total[:planes].reshape(planes // SUB, SUB, LANES) / divisor
    means_t = total[planes : 2 * planes].reshape(planes // SUB, SUB, LANES) / divisor
    bar_v = both_halves(jnp.sum(means_v, axis=0)) * (1.0 / snapshots)
    bar_t = both_halves(jnp.sum(means_t, axis=0)) * (1.0 / snapshots)

    def bar_copy(block, device, n):
        return pltpu.make_async_remote_copy(
            src_ref=bars.at[block], dst_ref=bars.at[block],
            send_sem=bar_send.at[n], recv_sem=bar_recv.at[block],
            device_id=(lat, device), device_id_type=MESH,
        )

    leads = lax.rem(me, owners) == 0

    @pl.when(leads)
    def _():
        bars[pl.ds(own_block, 1)] = bar_t[None]
        for d in range(1, lon_devices):
            bar_copy(own_block, lax.rem(me + d, lon_devices), d).start()

    swing = both_halves(jnp.sum((means_v - bar_v) * (means_t - bar_t), axis=0)) * (1.0 / snapshots)
    upper = jnp.where(sub < levels, scaling * count * bar_v * bar_t, scaling * count * swing)
    lower = scaling * total[2 * planes + SUB : 2 * planes + 2 * SUB] - upper
    if owners > 1:
        shift = LANES - lax.rem(me, owners) * share_rows
        upper = pltpu.roll(upper, shift, 1)
        lower = pltpu.roll(lower, shift, 1)
    for n in range(BASINS):
        lanes = slice(n * SUB, n * SUB + share_rows)
        transport_ref[0, n] = upper[:levels, lanes]
        transport_ref[1, n] = lower[:levels, lanes]
        transport_ref[2, n] = upper[levels:, lanes]
        transport_ref[3, n] = lower[levels:, lanes]

    for b in range(blocks):
        @pl.when(jnp.logical_or(own_block != b, jnp.logical_not(leads)))
        def _():
            bar_copy(b, b * owners, 0).wait_recv()
        at = pl.ds(b * SUB, SUB)
        wet = wet_cells(b)
        index = label_ref[at, :] * SUB + sub
        bar = bars[b]
        for k in range(levels):
            cells = jnp.take_along_axis(
                jnp.broadcast_to(bar[k : k + 1], (SUB, LANES)), index, axis=1
            )
            eddy_ref[k, at, :] = wet[k] * (average[k, at, :] - cells)

    @pl.when(lat > 0)
    def _():
        for copy in halo_copies():
            copy.wait_send()

    for b in range(blocks):
        for g in range(owners):
            @pl.when(b * owners + g != me)
            def _():
                stat_copy(b, g).wait_send()

    @pl.when(leads)
    def _():
        for d in range(1, lon_devices):
            bar_copy(own_block, lax.rem(me + d, lon_devices), d).wait_send()


def shards(
    lat_devices, lon_devices,
    poleward_flow, potential_warmth, water_profile_flag, floor_count, catchment_label_for_site,
):
    snapshots, levels, rows, columns = poleward_flow.shape
    share_rows = rows // lon_devices
    blocks = rows // SUB
    planes = snapshots * levels
    owners = SUB // share_rows
    fields = 2 * planes + 4 * levels
    f32, vmem, dma = jnp.float32, pltpu.VMEM, pltpu.SemaphoreType.DMA
    return pl.pallas_call(
        functools.partial(kernel, lat_devices, lon_devices, snapshots, levels, share_rows),
        out_shape=(
            jax.ShapeDtypeStruct((levels, rows, columns), f32),
            jax.ShapeDtypeStruct((4, BASINS, levels, share_rows), f32),
        ),
        in_specs=[pl.BlockSpec(memory_space=pl.ANY)] * 2 + [pl.BlockSpec(memory_space=vmem)] * 3,
        out_specs=(pl.BlockSpec(memory_space=vmem), pl.BlockSpec(memory_space=vmem)),
        scratch_shapes=[
            vmem((planes, rows, columns), f32),
            vmem((planes, rows + SUB, columns), f32),
            vmem((SUB, columns), jnp.int32),
            vmem((SUB, columns), jnp.int32),
            vmem((levels, rows, columns), f32),
            vmem((fields * SUB, LANES), f32),
            vmem((blocks, fields, LANES), f32),
            vmem((lon_devices, fields, LANES), f32),
            vmem((blocks, SUB, LANES), f32),
            dma((blocks,)),
            dma((blocks,)),
            dma((3,)),
            dma((3,)),
            dma((blocks, owners)),
            dma((lon_devices,)),
            dma((lon_devices,)),
            dma((blocks,)),
        ],
        compiler_params=pltpu.CompilerParams(collective_id=0, has_side_effects=True),
        name="heat_transport",
    )(
        poleward_flow.reshape(planes, rows, columns),
        potential_warmth.reshape(planes, rows, columns),
        water_profile_flag,
        floor_count,
        catchment_label_for_site,
    )


def solution(mesh):
    return jax.shard_map(
        functools.partial(shards, mesh.shape["lat"], mesh.shape["lon"]),
        mesh=mesh,
        in_specs=(
            P(None, None, "lat", "lon"),
            P(None, None, "lat", "lon"),
            P("lat", "lon"),
            P("lat", "lon"),
            P("lat", "lon"),
        ),
        out_specs=(P(None, "lat", "lon"), P(None, None, None, ("lat", "lon"))),
        check_vma=False,
    )
```

time: 108 us -> 22.5 us (0.21)
  blocking collectives: 28.2 us -> 0 us
  waiting for transfers between devices: 21.5 us -> 0 us
  Pallas kernels: 0 us -> 18.3 us
  matrix products: 18.2 us -> 0 us
  between operations: 14.3 us -> 0.64 us
  other arithmetic: 11.9 us -> 0 us
  local copies, waits for them, and re-layouts: 11.3 us -> 3.24 us
  starting transfers between devices: 2.62 us -> 0 us
    psum x1 -> x0, blocking collectives: 28.2 us -> none  [shards(): totals = lax.psum((stats[0], stats[1], stats[2]), 'lon')]
    psum x1 -> x0, waiting for transfers between devices: 19 us -> none  [shards(): totals = lax.psum((stats[0], stats[1], stats[2]), 'lon')]
    pallas_call x0 -> x1, Pallas kernels: none -> 18.3 us  [shards(): pl.pallas_call(functools.partial(kernel, lat_devices, lon_devices, snapsh...]
    dot_general x5 -> x0, matrix products: 18.2 us -> none  [the longest x1 5.38 us: shards(): jnp.einsum('yalq,falq->fyal', scaling_factors, poleward_flow, precision=h...]
    reduce_sum x7 -> x0, other arithmetic: 6.06 us -> none  [the longest x1 2.58 us: shards(): average_warmth = jnp.mean(warmth_entry, axis=0)]
    transpose x2 -> x0, local copies, waits for them, and re-layouts: 5.15 us -> none  [the longest x1 2.91 us: shards(): jnp.einsum('yalq,falq->fyal', scaling_factors, warmth_entry, precision=hi...]
    slice x3 -> x0, local copies, waits for them, and re-layouts: 3.56 us -> none  [the longest x1 2.53 us: shards(): potential_warmth[:, :, 1:, :]]
    ppermute x2 -> x0, starting transfers between devices: 2.58 us -> none  [shifted(): return lax.ppermute(block, axis, route)]
  transfers between devices with their start and end apart: 3 -> 0, of which waited for: 2 -> 0; matrix products, arithmetic and copies ran while one was open for 21% -> 0% of each run, Pallas kernels for 0% -> 0%
where the time goes in v1:
time: 22.5 us; the launch traced here: 22.2 us
  Pallas kernels  18.3 us (81%)
  local copies, waits for them, and re-layouts  3.24 us (14%)
  between operations  0.64 us (3%)
    pallas_call x1, Pallas kernels, shards(): pl.pallas_call(functools.partial(kernel, lat_devices, lon_devices, snapsh...  18.3 us
    pallas_call x1, local copies, waits for them, and re-layouts, shards(): pl.pallas_call(functools.partial(kernel, lat_devices, lon_devices, snapsh...  1.68 us
    unnamed x1, local copies, waits for them, and re-layouts  1.57 us

profile of v1, /device:TPU:0, one launch (start us, length us, event | category | flops | bytes accessed | tf_op | source)
XLA Modules:
  0.0 22.2 jit_solution(15050434622778690321)
XLA Ops:
  0.6 18.3 %heat_transport.1 = (f32[4,64,128]{2,1,0:T(8,128)}, f32[4,10,4,8]{3,2,1,0:T(4,128)}) custom-call(f32[40,64,128]{2,1,0:T(8,128)} %bitcast.2, f32[40,64,128]{2,1,0:T(8,128)} %bitcast.3, s32[64,128]{1,0:T(8,128)} %flag_ref.1, s32[64,128]{1,0:T(8,128)} %floor_ref.1, s32[64,128]{1,0:T(8,128)} %label_ref.1), custom_call_target="tpu_custom_call" | custom-call | tf_op jit(solution)/shard_map/heat_transport/pallas_call | solution.py:263
  19.0 1.7 %copy.7 = f32[4,10,4,8]{1,3,2,0:T(8,128)} copy(f32[4,10,4,8]{3,2,1,0:T(4,128)} %get-tuple-element.3) | data formatting | bytes 10240 | tf_op jit(solution)/shard_map/heat_transport/pallas_call | solution.py:263
  20.7 1.6 %copy.9 = f32[4,64,128]{2,1,0:T(8,128)} copy(f32[4,64,128]{2,1,0:T(8,128)} %get-tuple-element.6) | data formatting | bytes 262144

commit v2 on v1

--- a/solution.py
+++ b/solution.py
@@ -16,10 +16,11 @@
 
 def kernel(
     lat_devices, lon_devices, snapshots, levels, share_rows,
-    flow_hbm, warmth_hbm, flag_ref, floor_ref, label_ref,
+    flow_hbm, warmth_hbm, flag_hbm, floor_hbm, label_hbm,
     eddy_ref, transport_ref,
-    flow, warmth, halo_flag, halo_floor, average, dots, stats, received, bars,
-    load_flow, load_warmth, halo_send, halo_recv, stat_send, stat_recv, bar_send, bar_recv,
+    flag_ref, floor_ref, label_ref,
+    flow, warmth, average, dots, stats, received, bars,
+    load_flow, load_warmth, load_columns, halo_send, halo_recv, stat_send, stat_recv, bar_send, bar_recv,
 ):
     rows = flow.shape[1]
     blocks = rows // SUB
@@ -30,17 +31,31 @@
     own_block = me // owners
     scaling = 1.0 / math.sqrt(LANES * lon_devices)
 
+    def block_at(s):
+        late = own_block + 2 == blocks
+        s = jnp.where(jnp.logical_and(late, s < 2), 1 - s, s)
+        return lax.rem(own_block + 1 + s, blocks)
+
     def flow_copy(b):
-        at = pl.ds(b * SUB, SUB)
+        at = pl.ds(pl.multiple_of(b * SUB, SUB), SUB)
         return pltpu.make_async_copy(flow_hbm.at[:, at, :], flow.at[:, at, :], load_flow.at[b])
 
     def warmth_copy(b):
         at = pl.ds(b * SUB, SUB)
         return pltpu.make_async_copy(warmth_hbm.at[:, at, :], warmth.at[:, at, :], load_warmth.at[b])
 
+    columns = [
+        pltpu.make_async_copy(src, dst, load_columns.at[n])
+        for n, (src, dst) in enumerate(
+            ((flag_hbm, flag_ref.at[pl.ds(0, rows), :]), (floor_hbm, floor_ref.at[pl.ds(0, rows), :]), (label_hbm, label_ref))
+        )
+    ]
+    for copy in columns:
+        copy.start()
     for b in range(blocks):
         warmth_copy(b).start()
-        flow_copy(b).start()
+    for s in range(blocks):
+        flow_copy(block_at(s)).start()
 
     barrier = pltpu.get_barrier_semaphore()
     for d in range(1, lon_devices):
@@ -64,8 +79,8 @@
     def halo_copies():
         pairs = (
             (warmth.at[:, pl.ds(0, 1), :], warmth.at[:, pl.ds(rows, 1), :]),
-            (flag_ref.at[pl.ds(0, SUB), :], halo_flag),
-            (floor_ref.at[pl.ds(0, SUB), :], halo_floor),
+            (flag_ref.at[pl.ds(0, SUB), :], flag_ref.at[pl.ds(rows, SUB), :]),
+            (floor_ref.at[pl.ds(0, SUB), :], floor_ref.at[pl.ds(rows, SUB), :]),
         )
         return [
             pltpu.make_async_remote_copy(
@@ -75,25 +90,21 @@
             for n, (src, dst) in enumerate(pairs)
         ]
 
+    for copy in columns:
+        copy.wait()
     for b in range(blocks):
         warmth_copy(b).wait()
-        if b == 0:
-            @pl.when(lat > 0)
-            def _():
-                for copy in halo_copies():
-                    copy.start()
-        flow_copy(b).wait()
-
-    @pl.when(lat < lat_devices - 1)
+
+    @pl.when(lat > 0)
     def _():
         for copy in halo_copies():
-            copy.wait_recv()
+            copy.start()
 
     @pl.when(lat == lat_devices - 1)
     def _():
         warmth[:, pl.ds(rows, 1), :] = jnp.zeros((planes, 1, LANES), jnp.float32)
-        halo_flag[...] = jnp.zeros_like(halo_flag)
-        halo_floor[...] = jnp.zeros_like(halo_floor)
+        flag_ref[pl.ds(rows, SUB), :] = jnp.zeros((SUB, LANES), jnp.int32)
+        floor_ref[pl.ds(rows, SUB), :] = jnp.zeros((SUB, LANES), jnp.int32)
 
     sub = lax.broadcasted_iota(jnp.int32, (SUB, LANES), 0)
     level = lax.broadcasted_iota(jnp.int32, (levels, SUB, LANES), 0)
@@ -105,11 +116,10 @@
 
     def wet_cells(b):
         at = pl.ds(pl.multiple_of(b * SUB, SUB), SUB)
-        after = pl.ds(pl.multiple_of(lax.min(b + 1, blocks - 1) * SUB, SUB), SUB)
+        after = pl.ds(pl.multiple_of(b * SUB + SUB, SUB), SUB)
         depth = flag_ref[at, :] * floor_ref[at, :]
         inner = flag_ref[after, :] * floor_ref[after, :]
-        outer = halo_flag[...] * halo_floor[...]
-        limit = jnp.minimum(depth, next_row(depth, jnp.where(b == blocks - 1, outer, inner)))
+        limit = jnp.minimum(depth, next_row(depth, inner))
         return (level < limit[None]).astype(jnp.float32)
 
     def stat_copy(b, g):
@@ -120,7 +130,14 @@
         )
 
     def block_stats(s, carry):
-        b = lax.rem(own_block + 1 + s, blocks)
+        b = block_at(s)
+
+        @pl.when(jnp.logical_and(b == blocks - 1, lat < lat_devices - 1))
+        def _():
+            for copy in halo_copies():
+                copy.wait_recv()
+
+        flow_copy(b).wait()
         at = pl.ds(pl.multiple_of(b * SUB, SUB), SUB)
         after = pl.ds(pl.multiple_of(b * SUB + SUB, SUB), SUB)
         wet = wet_cells(b)
@@ -211,12 +228,14 @@
         shift = LANES - lax.rem(me, owners) * share_rows
         upper = pltpu.roll(upper, shift, 1)
         lower = pltpu.roll(lower, shift, 1)
-    for n in range(BASINS):
-        lanes = slice(n * SUB, n * SUB + share_rows)
-        transport_ref[0, n] = upper[:levels, lanes]
-        transport_ref[1, n] = lower[:levels, lanes]
-        transport_ref[2, n] = upper[levels:, lanes]
-        transport_ref[3, n] = lower[levels:, lanes]
+    spread = lax.rem(lax.broadcasted_iota(jnp.int32, (SUB, LANES), 1) * SUB + sub, LANES)
+    for c, part in enumerate((upper, lower, upper, lower)):
+        for k in range(levels):
+            row = c // 2 * levels + k
+            table = jnp.take_along_axis(
+                jnp.broadcast_to(part[row : row + 1], (SUB, LANES)), spread, axis=1
+            )
+            transport_ref[c, k] = table[:share_rows, :BASINS]
 
     for b in range(blocks):
         @pl.when(jnp.logical_or(own_block != b, jnp.logical_not(leads)))
@@ -260,19 +279,20 @@
     owners = SUB // share_rows
     fields = 2 * planes + 4 * levels
     f32, vmem, dma = jnp.float32, pltpu.VMEM, pltpu.SemaphoreType.DMA
-    return pl.pallas_call(
+    eddy_temp, transport = pl.pallas_call(
         functools.partial(kernel, lat_devices, lon_devices, snapshots, levels, share_rows),
         out_shape=(
-            jax.ShapeDtypeStruct((levels, rows, columns), f32),
-            jax.ShapeDtypeStruct((4, BASINS, levels, share_rows), f32),
+            vmem((levels, rows, columns), f32),
+            vmem((4, levels, share_rows, BASINS), f32),
         ),
-        in_specs=[pl.BlockSpec(memory_space=pl.ANY)] * 2 + [pl.BlockSpec(memory_space=vmem)] * 3,
+        in_specs=[pl.BlockSpec(memory_space=pltpu.HBM)] * 5,
         out_specs=(pl.BlockSpec(memory_space=vmem), pl.BlockSpec(memory_space=vmem)),
         scratch_shapes=[
+            vmem((rows + SUB, columns), jnp.int32),
+            vmem((rows + SUB, columns), jnp.int32),
+            vmem((rows, columns), jnp.int32),
             vmem((planes, rows, columns), f32),
             vmem((planes, rows + SUB, columns), f32),
-            vmem((SUB, columns), jnp.int32),
-            vmem((SUB, columns), jnp.int32),
             vmem((levels, rows, columns), f32),
             vmem((fields * SUB, LANES), f32),
             vmem((blocks, fields, LANES), f32),
@@ -282,12 +302,13 @@
             dma((blocks,)),
             dma((3,)),
             dma((3,)),
+            dma((3,)),
             dma((blocks, owners)),
             dma((lon_devices,)),
             dma((lon_devices,)),
             dma((blocks,)),
         ],
-        compiler_params=pltpu.CompilerParams(collective_id=0, has_side_effects=True),
+        compiler_params=pltpu.CompilerParams(collective_id=0, has_side_effects=True, vmem_limit_bytes=62 * 1024 * 1024),
         name="heat_transport",
     )(
         poleward_flow.reshape(planes, rows, columns),
@@ -296,6 +317,7 @@
         floor_count,
         catchment_label_for_site,
     )
+    return eddy_temp, jnp.transpose(transport, (0, 3, 1, 2))
 
 
 def solution(mesh):

time: 22.5 us -> 19 us (0.84)
  local copies, waits for them, and re-layouts: 3.24 us -> 1.29 us
  Pallas kernels: 18.3 us -> 16.9 us
    pallas_call x1 -> x0, local copies, waits for them, and re-layouts: 1.68 us -> none  [shards(): pl.pallas_call(functools.partial(kernel, lat_devices, lon_devices, snapsh...]
    pallas_call x1, Pallas kernels: 18.3 us -> 16.9 us  [shards(): pl.pallas_call(functools.partial(kernel, lat_devices, lon_devices, snapsh...]
    unnamed x1 -> x2, local copies, waits for them, and re-layouts: 1.57 us -> 1.29 us
where the time goes in v2:
time: 19 us; the launch traced here: 18.9 us
  Pallas kernels  16.9 us (89%)
  local copies, waits for them, and re-layouts  1.29 us (7%)
  between operations  0.64 us (3%)
    pallas_call x1, Pallas kernels, shards(): pl.pallas_call(functools.partial(kernel, lat_devices, lon_devices, snapsh...  16.9 us
    unnamed x2, local copies, waits for them, and re-layouts  1.29 us

profile of v2, /device:TPU:0, one launch (start us, length us, event | category | flops | bytes accessed | tf_op | source)
XLA Modules:
  0.0 18.9 jit_solution(8097921671300149697)
XLA Ops:
  0.6 16.9 %heat_transport.1 = (f32[4,64,128]{2,1,0:T(8,128)S(1)}, f32[4,4,8,10]{3,2,1,0:T(8,128)S(1)}) custom-call(f32[40,64,128]{2,1,0:T(8,128)} %bitcast.4, f32[40,64,128]{2,1,0:T(8,128)} %bitcast.5, s32[64,128]{1,0:T(8,128)} %flag_hbm.1, s32[64,128]{1,0:T(8,128)} %floor_hbm.1, s32[64,128]{1,0:T(8,128)} %label_hbm.1), custom_call_target="tpu_custom_call" | custom-call | tf_op jit(solution)/shard_map/heat_transport/pallas_call | solution.py:282
  17.6 0.7 %copy.9 = f32[4,64,128]{2,1,0:T(8,128)} copy(f32[4,64,128]{2,1,0:T(8,128)S(1)} %get-tuple-element.6) | data formatting | bytes 262144
  18.2 0.6 %copy.10 = f32[4,10,4,8]{1,3,2,0:T(8,128)} copy(f32[4,10,4,8]{1,3,2,0:T(8,128)S(1)} %bitcast.3) | data formatting | bytes 10240

commit v3 on v2

v3 whole, which is shorter than its diff:
```python
import functools
import math

import jax
import jax.numpy as jnp
from jax import lax
from jax.experimental import pallas as pl
from jax.experimental.pallas import tpu as pltpu
from jax.sharding import PartitionSpec as P

BASINS = 10
MESH = pl.DeviceIdType.MESH
SUB = 8
LANES = 128


def kernel(
    lat_devices, lon_devices, snapshots, levels, share_rows,
    flow_hbm, warmth_hbm, flag_hbm, floor_hbm, label_hbm,
    eddy_ref, transport_ref,
    flag_ref, floor_ref, label_ref, depth, flow, warmth, average, dots,
    halo_out, halo_in, stats, received, sums, peer_sums,
    load_flow, load_warmth, load_columns, halo_send, halo_recv,
    stat_send, stat_recv, sum_send, sum_recv,
):
    rows = flow.shape[1]
    blocks = rows // SUB
    last = blocks - 1
    owners = SUB // share_rows
    planes = snapshots * levels
    packed = stats.shape[1]
    fields = dots.shape[0] // SUB
    used = BASINS * SUB
    lat = lax.axis_index("lat")
    me = lax.axis_index("lon")
    own_block = me // owners
    scaling = 1.0 / math.sqrt(LANES * lon_devices)

    def window(b):
        return pl.ds(pl.multiple_of(b * SUB, SUB), SUB)

    def flow_copy(b):
        at = window(b)
        return pltpu.make_async_copy(flow_hbm.at[:, at, :], flow.at[:, at, :], load_flow.at[b])

    def warmth_copy(b):
        at = window(b)
        return pltpu.make_async_copy(warmth_hbm.at[:, at, :], warmth.at[:, at, :], load_warmth.at[b])

    columns = [
        pltpu.make_async_copy(src, dst, load_columns.at[n])
        for n, (src, dst) in enumerate(
            ((flag_hbm, flag_ref), (floor_hbm, floor_ref), (label_hbm, label_ref))
        )
    ]
    for copy in columns:
        copy.start()
    for b in range(blocks):
        warmth_copy(b).start()
        flow_copy(b).start()

    barrier = pltpu.get_barrier_semaphore()

    def greet(d, carry):
        pl.semaphore_signal(
            barrier, inc=1, device_id=(lat, lax.rem(me + d, lon_devices)), device_id_type=MESH
        )
        return carry

    @pl.when(lat > 0)
    def _():
        pl.semaphore_signal(barrier, inc=1, device_id=(lat - 1, me), device_id_type=MESH)

    @pl.when(lat < lat_devices - 1)
    def _():
        pl.semaphore_signal(barrier, inc=1, device_id=(lat + 1, me), device_id_type=MESH)

    lax.fori_loop(1, lon_devices, greet, 0)

    halo_copy = pltpu.make_async_remote_copy(
        src_ref=halo_out, dst_ref=halo_in, send_sem=halo_send, recv_sem=halo_recv,
        device_id=(jnp.maximum(lat - 1, 0), me), device_id_type=MESH,
    )

    def sum_copy(to, source, part):
        span = pl.ds(0, last) if part == 0 else pl.ds(last, 1)
        return pltpu.make_async_remote_copy(
            src_ref=sums.at[span], dst_ref=peer_sums.at[source, span],
            send_sem=sum_send.at[part, to], recv_sem=sum_recv.at[part, source],
            device_id=(lat, to), device_id_type=MESH,
        )

    def stat_copy(b, to, source):
        return pltpu.make_async_remote_copy(
            src_ref=stats.at[b], dst_ref=received.at[source],
            send_sem=stat_send.at[to], recv_sem=stat_recv.at[source],
            device_id=(lat, to), device_id_type=MESH,
        )

    def each_peer(action):
        def step(d, carry):
            action(lax.rem(me + d, lon_devices))
            return carry

        lax.fori_loop(1, lon_devices, step, 0)

    sub = lax.broadcasted_iota(jnp.int32, (SUB, LANES), 0)
    level = lax.broadcasted_iota(jnp.int32, (levels, SUB, LANES), 0).astype(jnp.float32)

    def next_row(here, after):
        first = lax.broadcasted_iota(jnp.int32, here.shape, here.ndim - 2) == 0
        return pltpu.roll(jnp.where(first, after, here), SUB - 1, here.ndim - 2)

    def both_halves(x):
        return x + pltpu.roll(x, levels, 0)

    def wet_cells(b):
        here = depth[window(b), :]
        limit = jnp.minimum(here, next_row(here, depth[window(b + 1), :]))
        return (level < limit[None]).astype(jnp.float32)

    def block_stats(b, carry):
        at = window(b)
        wet = wet_cells(b)
        velocity = flow[:, at, :].reshape(snapshots, levels, SUB, LANES)
        here = warmth[:, at, :]
        point = (0.5 * (here + next_row(here, warmth[:, window(b + 1), :]))).reshape(
            snapshots, levels, SUB, LANES
        )
        mean_velocity = jnp.sum(velocity, axis=0) * (1.0 / snapshots)
        mean_warmth = jnp.sum(point, axis=0) * (1.0 / snapshots)
        cross = jnp.sum((velocity - mean_velocity) * (point - mean_warmth), axis=0) * (1.0 / snapshots)
        average[:, at, :] = mean_warmth
        values = jnp.concatenate(
            [
                (velocity * wet[None]).reshape(planes, SUB, LANES),
                (point * wet[None]).reshape(planes, SUB, LANES),
                wet,
                wet,
                mean_velocity * mean_warmth * wet,
                cross * wet,
            ],
            axis=0,
        ).reshape(-1, LANES)
        high = values.astype(jnp.bfloat16)
        low = (values - high.astype(jnp.float32)).astype(jnp.bfloat16)
        labels = label_ref[at, :]
        member = jnp.concatenate(
            [(labels == n).astype(jnp.float32) for n in range(LANES // SUB)], axis=0
        ).astype(jnp.bfloat16)
        dots[...] = lax.dot_general(
            jnp.concatenate([high, low], axis=1), jnp.concatenate([member, member], axis=1),
            (((1,), (1,)), ((), ())), preferred_element_type=jnp.float32,
        )
        row_of = lax.rem(lax.broadcasted_iota(jnp.int32, (fields, LANES), 1), SUB)
        zonal = dots[pl.ds(0, fields, stride=SUB), :]
        for j in range(1, SUB):
            zonal = jnp.where(row_of == j, dots[pl.ds(j, fields, stride=SUB), :], zonal)
        warmth_sum = both_halves(
            jnp.sum(zonal[planes : 2 * planes].reshape(planes // SUB, SUB, LANES), axis=0)
        )
        count = zonal[2 * planes : 2 * planes + SUB]
        sums[pl.ds(b, 1)] = jnp.where(sub < levels, warmth_sum, count)[None]
        half = packed // 2
        rest = zonal[packed:]
        spare = lax.broadcasted_iota(jnp.int32, (half, LANES), 1) >= used
        stats[pl.ds(b, 1)] = jnp.concatenate(
            [
                jnp.where(spare, pltpu.roll(rest, used, 1), zonal[:half]),
                jnp.where(spare, pltpu.roll(rest, 2 * used - LANES, 1), zonal[half:packed]),
            ],
            axis=0,
        )[None]
        return carry

    for copy in columns:
        copy.wait()
    depth[pl.ds(0, rows), :] = (flag_ref[...] * floor_ref[...]).astype(jnp.float32)
    for b in range(blocks):
        warmth_copy(b).wait()
    halo_out[pl.ds(0, planes), :] = warmth[:, 0, :]
    halo_out[pl.ds(planes, SUB), :] = depth[pl.ds(0, SUB), :]

    def early_block(b, carry):
        flow_copy(b).wait()
        return block_stats(b, carry)

    lax.fori_loop(0, last, early_block, 0)

    pl.semaphore_wait(
        barrier,
        lon_devices - 1 + (lat > 0).astype(jnp.int32) + (lat < lat_devices - 1).astype(jnp.int32),
    )

    @pl.when(lat > 0)
    def _():
        halo_copy.start()

    each_peer(lambda to: sum_copy(to, me, 0).start())

    def send_stats(to):
        @pl.when(to // owners < last)
        def _():
            stat_copy(to // owners, to, me).start()

    each_peer(send_stats)
    flow_copy(last).wait()

    @pl.when(lat < lat_devices - 1)
    def _():
        halo_copy.wait_recv()
        warmth[:, rows, :] = halo_in[pl.ds(0, planes), :]
        depth[pl.ds(rows, SUB), :] = halo_in[pl.ds(planes, SUB), :]

    @pl.when(lat == lat_devices - 1)
    def _():
        warmth[:, rows, :] = jnp.zeros((planes, LANES), jnp.float32)
        depth[pl.ds(rows, SUB), :] = jnp.zeros((SUB, LANES), jnp.float32)

    block_stats(last, 0)
    each_peer(lambda to: sum_copy(to, me, 1).start())

    def send_last(to):
        @pl.when(to // owners == last)
        def _():
            stat_copy(last, to, me).start()

    each_peer(send_last)

    def add_sums(d, total):
        source = lax.rem(me + lon_devices - d, lon_devices)
        sum_copy(me, source, 0).wait_recv()
        sum_copy(me, source, 1).wait_recv()
        return total + peer_sums[pl.ds(source, 1)][0]

    all_sums = lax.fori_loop(1, lon_devices, add_sums, sums[...])
    for b in range(blocks):
        at = pl.ds(b * SUB, SUB)
        wet = wet_cells(b)
        index = label_ref[at, :] * SUB + sub
        bar = all_sums[b] / jnp.maximum(pltpu.roll(all_sums[b], levels, 0), 1.0) * (1.0 / snapshots)
        for k in range(levels):
            cells = jnp.take_along_axis(
                jnp.broadcast_to(bar[k : k + 1], (SUB, LANES)), index, axis=1
            )
            eddy_ref[k, at, :] = wet[k] * (average[k, at, :] - cells)

    def add_received(d, total):
        source = lax.rem(me + lon_devices - d, lon_devices)
        stat_copy(0, me, source).wait_recv()
        return total + received[pl.ds(source, 1)][0]

    total = lax.fori_loop(1, lon_devices, add_received, stats[pl.ds(own_block, 1)][0])
    half = packed // 2
    lane = lax.broadcasted_iota(jnp.int32, (half, LANES), 1)
    total = jnp.concatenate(
        [
            total,
            jnp.where(
                lane < LANES - used,
                pltpu.roll(total[:half], LANES - used, 1),
                pltpu.roll(total[half:], 2 * LANES - 2 * used, 1),
            ),
        ],
        axis=0,
    )
    count = total[2 * planes : 2 * planes + SUB]
    divisor = jnp.maximum(count, 1.0)
    means_v = total[:planes].reshape(planes // SUB, SUB, LANES) / divisor
    means_t = total[planes : 2 * planes].reshape(planes // SUB, SUB, LANES) / divisor
    bar_v = both_halves(jnp.sum(means_v, axis=0)) * (1.0 / snapshots)
    bar_t = both_halves(jnp.sum(means_t, axis=0)) * (1.0 / snapshots)
    swing = both_halves(jnp.sum((means_v - bar_v) * (means_t - bar_t), axis=0)) * (1.0 / snapshots)
    upper = jnp.where(sub < levels, scaling * count * bar_v * bar_t, scaling * count * swing)
    lower = scaling * total[2 * planes + SUB : 2 * planes + 2 * SUB] - upper
    if owners > 1:
        shift = LANES - lax.rem(me, owners) * share_rows
        upper = pltpu.roll(upper, shift, 1)
        lower = pltpu.roll(lower, shift, 1)
    spread = lax.rem(lax.broadcasted_iota(jnp.int32, (SUB, LANES), 1) * SUB + sub, LANES)
    for c, part in enumerate((upper, lower, upper, lower)):
        for k in range(levels):
            row = c // 2 * levels + k
            table = jnp.take_along_axis(
                jnp.broadcast_to(part[row : row + 1], (SUB, LANES)), spread, axis=1
            )
            transport_ref[c, k] = table[:share_rows, :BASINS]

    @pl.when(lat > 0)
    def _():
        halo_copy.wait_send()

    def sent(to):
        sum_copy(to, me, 0).wait_send()
        sum_copy(to, me, 1).wait_send()
        stat_copy(to // owners, to, me).wait_send()

    each_peer(sent)


def shards(
    lat_devices, lon_devices,
    poleward_flow, potential_warmth, water_profile_flag, floor_count, catchment_label_for_site,
):
    snapshots, levels, rows, columns = poleward_flow.shape
    share_rows = rows // lon_devices
    blocks = rows // SUB
    planes = snapshots * levels
    fields = 2 * planes + 4 * levels
    packed = fields * 2 // 3
    f32, i32, vmem, dma = jnp.float32, jnp.int32, pltpu.VMEM, pltpu.SemaphoreType.DMA
    eddy_temp, transport = pl.pallas_call(
        functools.partial(kernel, lat_devices, lon_devices, snapshots, levels, share_rows),
        out_shape=(
            vmem((levels, rows, columns), f32),
            vmem((4, levels, share_rows, BASINS), f32),
        ),
        in_specs=[pl.BlockSpec(memory_space=pltpu.HBM)] * 5,
        out_specs=(pl.BlockSpec(memory_space=vmem), pl.BlockSpec(memory_space=vmem)),
        scratch_shapes=[
            vmem((rows, columns), i32),
            vmem((rows, columns), i32),
            vmem((rows, columns), i32),
            vmem((rows + SUB, columns), f32),
            vmem((planes, rows, columns), f32),
            vmem((planes, rows + SUB, columns), f32),
            vmem((levels, rows, columns), f32),
            vmem((fields * SUB, LANES), f32),
            vmem((planes + SUB, LANES), f32),
            vmem((planes + SUB, LANES), f32),
            vmem((blocks, packed, LANES), f32),
            vmem((lon_devices, packed, LANES), f32),
            vmem((blocks, SUB, LANES), f32),
            vmem((lon_devices, blocks, SUB, LANES), f32),
            dma((blocks,)),
            dma((blocks,)),
            dma((3,)),
            dma,
            dma,
            dma((lon_devices,)),
            dma((lon_devices,)),
            dma((2, lon_devices)),
            dma((2, lon_devices)),
        ],
        compiler_params=pltpu.CompilerParams(
            collective_id=0, has_side_effects=True, vmem_limit_bytes=62 * 1024 * 1024
        ),
        name="heat_transport",
    )(
        poleward_flow.reshape(planes, rows, columns),
        potential_warmth.reshape(planes, rows, columns),
        water_profile_flag,
        floor_count,
        catchment_label_for_site,
    )
    return eddy_temp, jnp.transpose(transport, (0, 3, 1, 2))


def solution(mesh):
    return jax.shard_map(
        functools.partial(shards, mesh.shape["lat"], mesh.shape["lon"]),
        mesh=mesh,
        in_specs=(
            P(None, None, "lat", "lon"),
            P(None, None, "lat", "lon"),
            P("lat", "lon"),
            P("lat", "lon"),
            P("lat", "lon"),
        ),
        out_specs=(P(None, "lat", "lon"), P(None, None, None, ("lat", "lon"))),
        check_vma=False,
    )
```

time: 19 us -> 17.7 us (0.932)
  Pallas kernels: 16.9 us -> 15.7 us
    pallas_call x1, Pallas kernels: 16.9 us -> 15.7 us  [shards(): pl.pallas_call(functools.partial(kernel, lat_devices, lon_devices, snapsh...]
where the time goes in v3:
time: 17.7 us; the launch traced here: 17.6 us
  Pallas kernels  15.7 us (89%)
  local copies, waits for them, and re-layouts  1.29 us (7%)
  between operations  0.64 us (4%)
    pallas_call x1, Pallas kernels, shards(): pl.pallas_call(functools.partial(kernel, lat_devices, lon_devices, snapsh...  15.7 us
    unnamed x2, local copies, waits for them, and re-layouts  1.29 us

profile of v3, /device:TPU:0, one launch (start us, length us, event | category | flops | bytes accessed | tf_op | source)
XLA Modules:
  0.0 17.6 jit_solution(9838559322060631296)
XLA Ops:
  0.6 15.7 %heat_transport.1 = (f32[4,64,128]{2,1,0:T(8,128)S(1)}, f32[4,4,8,10]{3,2,1,0:T(8,128)S(1)}) custom-call(f32[40,64,128]{2,1,0:T(8,128)} %bitcast.4, f32[40,64,128]{2,1,0:T(8,128)} %bitcast.5, s32[64,128]{1,0:T(8,128)} %flag_hbm.1, s32[64,128]{1,0:T(8,128)} %floor_hbm.1, s32[64,128]{1,0:T(8,128)} %label_hbm.1), custom_call_target="tpu_custom_call" | custom-call | tf_op jit(solution)/shard_map/heat_transport/pallas_call | solution.py:312
  16.3 0.7 %copy.9 = f32[4,64,128]{2,1,0:T(8,128)} copy(f32[4,64,128]{2,1,0:T(8,128)S(1)} %get-tuple-element.6) | data formatting | bytes 262144
  16.9 0.6 %copy.10 = f32[4,10,4,8]{1,3,2,0:T(8,128)} copy(f32[4,10,4,8]{1,3,2,0:T(8,128)S(1)} %bitcast.3) | data formatting | bytes 10240

commit v4 on v3

--- a/solution.py
+++ b/solution.py
@@ -19,9 +19,9 @@
     flow_hbm, warmth_hbm, flag_hbm, floor_hbm, label_hbm,
     eddy_ref, transport_ref,
     flag_ref, floor_ref, label_ref, depth, flow, warmth, average, dots,
-    halo_out, halo_in, stats, received, sums, peer_sums,
+    halo_out, halo_in, stats, received, sums, pair_sums, chip_sums, peer_sums, peer_last,
     load_flow, load_warmth, load_columns, halo_send, halo_recv,
-    stat_send, stat_recv, sum_send, sum_recv,
+    stat_send, stat_recv, pair_send, pair_recv, sum_send, sum_recv, last_send, last_recv,
 ):
     rows = flow.shape[1]
     blocks = rows // SUB
@@ -82,13 +82,33 @@
         device_id=(jnp.maximum(lat - 1, 0), me), device_id_type=MESH,
     )
 
-    def sum_copy(to, source, part):
-        span = pl.ds(0, last) if part == 0 else pl.ds(last, 1)
+    chips = lon_devices // 2
+    core = lax.rem(me, 2)
+    pair_copy = pltpu.make_async_remote_copy(
+        src_ref=sums.at[pl.ds(0, last)], dst_ref=pair_sums, send_sem=pair_send, recv_sem=pair_recv,
+        device_id=(lat, me + 1 - 2 * core), device_id_type=MESH,
+    )
+
+    def chip_copy(to, source):
         return pltpu.make_async_remote_copy(
-            src_ref=sums.at[span], dst_ref=peer_sums.at[source, span],
-            send_sem=sum_send.at[part, to], recv_sem=sum_recv.at[part, source],
+            src_ref=chip_sums, dst_ref=peer_sums.at[source],
+            send_sem=sum_send.at[to], recv_sem=sum_recv.at[source],
+            device_id=(lat, 2 * to + core), device_id_type=MESH,
+        )
+
+    def last_copy(to, source):
+        return pltpu.make_async_remote_copy(
+            src_ref=sums.at[last], dst_ref=peer_last.at[source],
+            send_sem=last_send.at[to], recv_sem=last_recv.at[source],
             device_id=(lat, to), device_id_type=MESH,
         )
+
+    def each_chip(action):
+        def step(d, carry):
+            action(lax.rem(me // 2 + d, chips))
+            return carry
+
+        lax.fori_loop(1, chips, step, 0)
 
     def stat_copy(b, to, source):
         return pltpu.make_async_remote_copy(
@@ -185,7 +205,7 @@
         flow_copy(b).wait()
         return block_stats(b, carry)
 
-    lax.fori_loop(0, last, early_block, 0)
+    lax.fori_loop(0, last // 2, early_block, 0)
 
     pl.semaphore_wait(
         barrier,
@@ -196,7 +216,8 @@
     def _():
         halo_copy.start()
 
-    each_peer(lambda to: sum_copy(to, me, 0).start())
+    lax.fori_loop(last // 2, last, early_block, 0)
+    pair_copy.start()
 
     def send_stats(to):
         @pl.when(to // owners < last)
@@ -204,6 +225,9 @@
             stat_copy(to // owners, to, me).start()
 
     each_peer(send_stats)
+    pair_copy.wait_recv()
+    chip_sums[...] = sums[pl.ds(0, last)] + pair_sums[...]
+    each_chip(lambda to: chip_copy(to, me // 2).start())
     flow_copy(last).wait()
 
     @pl.when(lat < lat_devices - 1)
@@ -218,7 +242,7 @@
         depth[pl.ds(rows, SUB), :] = jnp.zeros((SUB, LANES), jnp.float32)
 
     block_stats(last, 0)
-    each_peer(lambda to: sum_copy(to, me, 1).start())
+    each_peer(lambda to: last_copy(to, me).start())
 
     def send_last(to):
         @pl.when(to // owners == last)
@@ -227,23 +251,25 @@
 
     each_peer(send_last)
 
-    def add_sums(d, total):
-        source = lax.rem(me + lon_devices - d, lon_devices)
-        sum_copy(me, source, 0).wait_recv()
-        sum_copy(me, source, 1).wait_recv()
-        return total + peer_sums[pl.ds(source, 1)][0]
-
-    all_sums = lax.fori_loop(1, lon_devices, add_sums, sums[...])
-    for b in range(blocks):
+    def block_eddy(b, block_sums):
         at = pl.ds(b * SUB, SUB)
         wet = wet_cells(b)
         index = label_ref[at, :] * SUB + sub
-        bar = all_sums[b] / jnp.maximum(pltpu.roll(all_sums[b], levels, 0), 1.0) * (1.0 / snapshots)
+        bar = block_sums / jnp.maximum(pltpu.roll(block_sums, levels, 0), 1.0) * (1.0 / snapshots)
         for k in range(levels):
             cells = jnp.take_along_axis(
                 jnp.broadcast_to(bar[k : k + 1], (SUB, LANES)), index, axis=1
             )
             eddy_ref[k, at, :] = wet[k] * (average[k, at, :] - cells)
+
+    def add_sums(d, total):
+        source = lax.rem(me // 2 + chips - d, chips)
+        chip_copy(0, source).wait_recv()
+        return total + peer_sums[pl.ds(source, 1)][0]
+
+    first_sums = lax.fori_loop(1, chips, add_sums, chip_sums[...])
+    for b in range(last):
+        block_eddy(b, first_sums[b])
 
     def add_received(d, total):
         source = lax.rem(me + lon_devices - d, lon_devices)
@@ -286,13 +312,22 @@
             )
             transport_ref[c, k] = table[:share_rows, :BASINS]
 
+    def add_last(d, total):
+        source = lax.rem(me + lon_devices - d, lon_devices)
+        last_copy(0, source).wait_recv()
+        return total + peer_last[pl.ds(source, 1)][0]
+
+    block_eddy(last, lax.fori_loop(1, lon_devices, add_last, sums[last]))
+
     @pl.when(lat > 0)
     def _():
         halo_copy.wait_send()
 
+    pair_copy.wait_send()
+    each_chip(lambda to: chip_copy(to, me // 2).wait_send())
+
     def sent(to):
-        sum_copy(to, me, 0).wait_send()
-        sum_copy(to, me, 1).wait_send()
+        last_copy(to, me).wait_send()
         stat_copy(to // owners, to, me).wait_send()
 
     each_peer(sent)
@@ -331,7 +366,10 @@
             vmem((blocks, packed, LANES), f32),
             vmem((lon_devices, packed, LANES), f32),
             vmem((blocks, SUB, LANES), f32),
-            vmem((lon_devices, blocks, SUB, LANES), f32),
+            vmem((blocks - 1, SUB, LANES), f32),
+            vmem((blocks - 1, SUB, LANES), f32),
+            vmem((lon_devices // 2, blocks - 1, SUB, LANES), f32),
+            vmem((lon_devices, SUB, LANES), f32),
             dma((blocks,)),
             dma((blocks,)),
             dma((3,)),
@@ -339,8 +377,12 @@
             dma,
             dma((lon_devices,)),
             dma((lon_devices,)),
-            dma((2, lon_devices)),
-            dma((2, lon_devices)),
+            dma,
+            dma,
+            dma((lon_devices // 2,)),
+            dma((lon_devices // 2,)),
+            dma((lon_devices,)),
+            dma((lon_devices,)),
         ],
         compiler_params=pltpu.CompilerParams(
             collective_id=0, has_side_effects=True, vmem_limit_bytes=62 * 1024 * 1024

time: 17.7 us -> 16.2 us (0.915)
  Pallas kernels: 15.7 us -> 14.1 us
    pallas_call x1, Pallas kernels: 15.7 us -> 14.1 us  [shards(): pl.pallas_call(functools.partial(kernel, lat_devices, lon_devices, snapsh...]
where the time goes in v4:
time: 16.2 us; the launch traced here: 16 us
  Pallas kernels  14.1 us (87%)
  local copies, waits for them, and re-layouts  1.29 us (8%)
  between operations  0.64 us (4%)
    pallas_call x1, Pallas kernels, shards(): pl.pallas_call(functools.partial(kernel, lat_devices, lon_devices, snapsh...  14.1 us
    unnamed x2, local copies, waits for them, and re-layouts  1.29 us

profile of v4, /device:TPU:0, one launch (start us, length us, event | category | flops | bytes accessed | tf_op | source)
XLA Modules:
  0.0 16.0 jit_solution(3948752205070913541)
XLA Ops:
  0.6 14.1 %heat_transport.1 = (f32[4,64,128]{2,1,0:T(8,128)S(1)}, f32[4,4,8,10]{3,2,1,0:T(8,128)S(1)}) custom-call(f32[40,64,128]{2,1,0:T(8,128)} %bitcast.4, f32[40,64,128]{2,1,0:T(8,128)} %bitcast.5, s32[64,128]{1,0:T(8,128)} %flag_hbm.1, s32[64,128]{1,0:T(8,128)} %floor_hbm.1, s32[64,128]{1,0:T(8,128)} %label_hbm.1), custom_call_target="tpu_custom_call" | custom-call | tf_op jit(solution)/shard_map/heat_transport/pallas_call | solution.py:347
  14.7 0.7 %copy.9 = f32[4,64,128]{2,1,0:T(8,128)} copy(f32[4,64,128]{2,1,0:T(8,128)S(1)} %get-tuple-element.6) | data formatting | bytes 262144
  15.4 0.6 %copy.10 = f32[4,10,4,8]{1,3,2,0:T(8,128)} copy(f32[4,10,4,8]{1,3,2,0:T(8,128)S(1)} %bitcast.3) | data formatting | bytes 10240

commit v5 on v4

--- a/solution.py
+++ b/solution.py
@@ -29,7 +29,7 @@
     owners = SUB // share_rows
     planes = snapshots * levels
     packed = stats.shape[1]
-    fields = dots.shape[0] // SUB
+    fields = dots.shape[1] // SUB
     used = BASINS * SUB
     lat = lax.axis_index("lat")
     me = lax.axis_index("lon")
@@ -168,14 +168,14 @@
         member = jnp.concatenate(
             [(labels == n).astype(jnp.float32) for n in range(LANES // SUB)], axis=0
         ).astype(jnp.bfloat16)
-        dots[...] = lax.dot_general(
+        dots[b] = lax.dot_general(
             jnp.concatenate([high, low], axis=1), jnp.concatenate([member, member], axis=1),
             (((1,), (1,)), ((), ())), preferred_element_type=jnp.float32,
         )
         row_of = lax.rem(lax.broadcasted_iota(jnp.int32, (fields, LANES), 1), SUB)
-        zonal = dots[pl.ds(0, fields, stride=SUB), :]
+        zonal = dots[b, pl.ds(0, fields, stride=SUB), :]
         for j in range(1, SUB):
-            zonal = jnp.where(row_of == j, dots[pl.ds(j, fields, stride=SUB), :], zonal)
+            zonal = jnp.where(row_of == j, dots[b, pl.ds(j, fields, stride=SUB), :], zonal)
         warmth_sum = both_halves(
             jnp.sum(zonal[planes : 2 * planes].reshape(planes // SUB, SUB, LANES), axis=0)
         )
@@ -205,7 +205,10 @@
         flow_copy(b).wait()
         return block_stats(b, carry)
 
-    lax.fori_loop(0, last // 2, early_block, 0)
+    for b in range(blocks):
+        flow_copy(b).wait()
+    for b in range(last // 2):
+        block_stats(b, 0)
 
     pl.semaphore_wait(
         barrier,
@@ -216,7 +219,8 @@
     def _():
         halo_copy.start()
 
-    lax.fori_loop(last // 2, last, early_block, 0)
+    for b in range(last // 2, last):
+        block_stats(b, 0)
     pair_copy.start()
 
     def send_stats(to):
@@ -228,7 +232,6 @@
     pair_copy.wait_recv()
     chip_sums[...] = sums[pl.ds(0, last)] + pair_sums[...]
     each_chip(lambda to: chip_copy(to, me // 2).start())
-    flow_copy(last).wait()
 
     @pl.when(lat < lat_devices - 1)
     def _():
@@ -360,7 +363,7 @@
             vmem((planes, rows, columns), f32),
             vmem((planes, rows + SUB, columns), f32),
             vmem((levels, rows, columns), f32),
-            vmem((fields * SUB, LANES), f32),
+            vmem((blocks, fields * SUB, LANES), f32),
             vmem((planes + SUB, LANES), f32),
             vmem((planes + SUB, LANES), f32),
             vmem((blocks, packed, LANES), f32),

time: 16.2 us -> 15.2 us (0.938)
  Pallas kernels: 14.1 us -> 13.1 us
    pallas_call x1, Pallas kernels: 14.1 us -> 13.1 us  [shards(): pl.pallas_call(functools.partial(kernel, lat_devices, lon_devices, snapsh...]
where the time goes in v5:
time: 15.2 us; the launch traced here: 15.1 us
  Pallas kernels  13.1 us (86%)
  local copies, waits for them, and re-layouts  1.29 us (8%)
  between operations  0.64 us (4%)
    pallas_call x1, Pallas kernels, shards(): pl.pallas_call(functools.partial(kernel, lat_devices, lon_devices, snapsh...  13.1 us
    unnamed x2, local copies, waits for them, and re-layouts  1.29 us

profile of v5, /device:TPU:0, one launch (start us, length us, event | category | flops | bytes accessed | tf_op | source)
XLA Modules:
  0.0 15.1 jit_solution(3097470480676556169)
XLA Ops:
  0.6 13.1 %heat_transport.1 = (f32[4,64,128]{2,1,0:T(8,128)S(1)}, f32[4,4,8,10]{3,2,1,0:T(8,128)S(1)}) custom-call(f32[40,64,128]{2,1,0:T(8,128)} %bitcast.4, f32[40,64,128]{2,1,0:T(8,128)} %bitcast.5, s32[64,128]{1,0:T(8,128)} %flag_hbm.1, s32[64,128]{1,0:T(8,128)} %floor_hbm.1, s32[64,128]{1,0:T(8,128)} %label_hbm.1), custom_call_target="tpu_custom_call" | custom-call | tf_op jit(solution)/shard_map/heat_transport/pallas_call | solution.py:350
  13.8 0.7 %copy.9 = f32[4,64,128]{2,1,0:T(8,128)} copy(f32[4,64,128]{2,1,0:T(8,128)S(1)} %get-tuple-element.6) | data formatting | bytes 262144
  14.4 0.6 %copy.10 = f32[4,10,4,8]{1,3,2,0:T(8,128)} copy(f32[4,10,4,8]{1,3,2,0:T(8,128)S(1)} %bitcast.3) | data formatting | bytes 10240
